TPU v7x, 256 devices: a whole 4x4x8 slice. The times are simulated.
256 devices in a mesh: section: 16 (over z_lo, x), tensor: 16 (over z_hi, y, core).
Axes of the slice: x: 4, y: 4, z: 8 (z_hi: 2, z_lo: 4; z = z_hi * 4 + z_lo), core: 2. Of those that a mesh axis runs over, the one named last changes fastest.
Arguments:
- layer_input: bfloat16 [6144, 5120], P('section', 'tensor'), may hold values from -6 to 6
- query_rows: bfloat16 [6144, 4096], P('section', 'tensor'), may hold values from -4.6 to 4.6
- key_rows: bfloat16 [6144, 4096], P('section', 'tensor'), may hold values from -4.6 to 4.6
- value_rows: bfloat16 [6144, 4096], P('section', 'tensor'), may hold values from -6 to 6
- out_grad: bfloat16 [6144, 5120], P('section', 'tensor'), may hold values from -6 to 6
- window: int32 [32], P('tensor'), may hold values from 96 to 192, as said below
- w_query: bfloat16 [5120, 4096], P(None, 'tensor'), may hold values from -0.078125 to 0.078125
- w_key: bfloat16 [5120, 4096], P(None, 'tensor'), may hold values from -0.078125 to 0.078125
- w_value: bfloat16 [5120, 4096], P(None, 'tensor'), may hold values from -0.078125 to 0.078125
- w_out: bfloat16 [4096, 5120], P('tensor'), may hold values from -0.09375 to 0.09375
Outputs:
- input_grad: bfloat16 [6144, 5120], P('section', 'tensor')
- query_weight_grad: float32 [5120, 4096], P('section', 'tensor')
- key_weight_grad: float32 [5120, 4096], P('section', 'tensor')
- value_weight_grad: float32 [5120, 4096], P('section', 'tensor')
- out_weight_grad: float32 [4096, 5120], P('tensor', 'section')
Inputs may be any that keep to these rules, and one draw needn't show every extreme that they name: `window`: the number of most recent positions, the query's own included, that a head sees; some head has exactly 192.
All inputs are finite; a program needn't handle non-finite values.
Results may differ from a plain program's by a relative error of at most 0.025.
Values may be sent and summed in bfloat16 or wider, within the bound.
A program may use at most 128 MiB of HBM per device.

v0:
```python
import math

import jax
import jax.numpy as jnp
from jax import lax
from jax.sharding import PartitionSpec as P

HD = 128
WMAX = 192


def from_behind(x, axis, by):
    length = lax.axis_size(axis)
    pairs = [(i, i + by) for i in range(length) if 0 <= i + by < length]
    return lax.ppermute(x, axis, pairs)


def window_backward(query_rows, key_rows, value_rows, grad_rows, window, first_row):
    row_count = query_rows.shape[0]
    key_count = key_rows.shape[0]
    span = key_count - row_count
    head_count = query_rows.shape[1] // HD
    scaling = 1.0 / math.sqrt(HD)
    query_heads = query_rows.reshape(row_count, head_count, HD)
    key_heads = key_rows.reshape(key_count, head_count, HD)
    value_heads = value_rows.reshape(key_count, head_count, HD)
    grad_heads = grad_rows.reshape(row_count, head_count, HD)
    query_pos = first_row + jnp.arange(row_count, dtype=jnp.int32)
    key_pos = first_row - span + jnp.arange(key_count, dtype=jnp.int32)
    distance = query_pos[:, None] - key_pos[None, :]
    visible = (
        (distance[None] >= 0)
        & (distance[None] < window[:, None, None])
        & (key_pos[None, None, :] >= 0)
    )
    scores = (
        jnp.einsum("thd,khd->htk", query_heads, key_heads, preferred_element_type=jnp.float32)
        * scaling
    )
    scores = jnp.where(visible, scores, -jnp.inf)
    row_max = jnp.max(scores, axis=2, keepdims=True)
    expon = jnp.exp(scores - row_max)
    probs = expon / jnp.sum(expon, axis=2, keepdims=True)
    probs_low = probs.astype(jnp.bfloat16)
    attended = jnp.einsum(
        "htk,khd->thd", probs_low, value_heads, preferred_element_type=jnp.float32
    ).astype(jnp.bfloat16)
    prob_grad = jnp.einsum(
        "thd,khd->htk", grad_heads, value_heads, preferred_element_type=jnp.float32
    )
    row_term = jnp.sum(grad_heads.astype(jnp.float32) * attended.astype(jnp.float32), axis=2)
    score_grad = (probs * (prob_grad - jnp.transpose(row_term)[:, :, None])).astype(jnp.bfloat16)
    grad_query = (
        jnp.einsum("htk,khd->thd", score_grad, key_heads, preferred_element_type=jnp.float32)
        * scaling
    )
    grad_key = (
        jnp.einsum("htk,thd->khd", score_grad, query_heads, preferred_element_type=jnp.float32)
        * scaling
    )
    grad_value = jnp.einsum(
        "htk,thd->khd", probs_low, grad_heads, preferred_element_type=jnp.float32
    )
    cols = head_count * HD
    return (
        attended.reshape(row_count, cols),
        grad_query.reshape(row_count, cols),
        grad_key.reshape(key_count, cols),
        grad_value.reshape(key_count, cols),
    )


def local(
    layer_input, query_rows, key_rows, value_rows, out_grad, window, w_query, w_key, w_value, w_out
):
    by_cols = (((1,), (1,)), ((), ()))
    by_rows = (((0,), (0,)), ((), ()))
    full_input, full_grad = (
        lax.all_gather(layer_input, "tensor", axis=1, tiled=True),
        lax.all_gather(out_grad, "tensor", axis=1, tiled=True),
    )
    head_grad = lax.dot_general(
        full_grad, w_out, by_cols, preferred_element_type=jnp.float32
    ).astype(jnp.bfloat16)
    row_count = query_rows.shape[0]
    cycle_keys, cycle_values = from_behind(
        (key_rows[row_count - WMAX :], value_rows[row_count - WMAX :]), "section", 1
    )
    first_row = lax.axis_index("section") * row_count
    attended, grad_query, key_all, value_all = window_backward(
        query_rows,
        jnp.concatenate([cycle_keys, key_rows], axis=0),
        jnp.concatenate([cycle_values, value_rows], axis=0),
        head_grad,
        window,
        first_row,
    )
    carried_keys, carried_values = (
        from_behind(key_all[:WMAX].astype(jnp.bfloat16), "section", -1).astype(jnp.float32),
        from_behind(value_all[:WMAX].astype(jnp.bfloat16), "section", -1).astype(jnp.float32),
    )
    query_grad = grad_query.astype(jnp.bfloat16)
    key_grad = key_all[WMAX:].at[row_count - WMAX :].add(carried_keys).astype(jnp.bfloat16)
    value_grad = value_all[WMAX:].at[row_count - WMAX :].add(carried_values).astype(jnp.bfloat16)
    partial_sum = lax.dot_general(query_grad, w_query, by_cols, preferred_element_type=jnp.float32)
    partial_sum = partial_sum + lax.dot_general(
        key_grad, w_key, by_cols, preferred_element_type=jnp.float32
    )
    partial_sum = partial_sum + lax.dot_general(
        value_grad, w_value, by_cols, preferred_element_type=jnp.float32
    )
    input_grad = lax.psum_scatter(
        partial_sum.astype(jnp.bfloat16), "tensor", scatter_dimension=1, tiled=True
    )
    part_query = lax.dot_general(
        full_input, query_grad, by_rows, preferred_element_type=jnp.float32
    )
    part_key = lax.dot_general(full_input, key_grad, by_rows, preferred_element_type=jnp.float32)
    part_value = lax.dot_general(
        full_input, value_grad, by_rows, preferred_element_type=jnp.float32
    )
    query_weight_grad, key_weight_grad, value_weight_grad = (
        lax.psum_scatter(
            part_query.astype(jnp.bfloat16), "section", scatter_dimension=0, tiled=True
        ).astype(jnp.float32),
        lax.psum_scatter(
            part_key.astype(jnp.bfloat16), "section", scatter_dimension=0, tiled=True
        ).astype(jnp.float32),
        lax.psum_scatter(
            part_value.astype(jnp.bfloat16), "section", scatter_dimension=0, tiled=True
        ).astype(jnp.float32),
    )
    part_out = lax.dot_general(attended, full_grad, by_rows, preferred_element_type=jnp.float32)
    out_weight_grad = lax.psum_scatter(
        part_out.astype(jnp.bfloat16), "section", scatter_dimension=1, tiled=True
    ).astype(jnp.float32)
    return (input_grad, query_weight_grad, key_weight_grad, value_weight_grad, out_weight_grad)


def solution(mesh):
    in_specs = (
        P("section", "tensor"),
        P("section", "tensor"),
        P("section", "tensor"),
        P("section", "tensor"),
        P("section", "tensor"),
        P("tensor"),
        P(None, "tensor"),
        P(None, "tensor"),
        P(None, "tensor"),
        P("tensor", None),
    )
    out_specs = (
        P("section", "tensor"),
        P("section", "tensor"),
        P("section", "tensor"),
        P("section", "tensor"),
        P("tensor", "section"),
    )
    return jax.shard_map(local, mesh=mesh, in_specs=in_specs, out_specs=out_specs, check_vma=False)
```

profile of v0, /device:TPU:33, one launch (start us, length us, event | category | flops | bytes accessed | tf_op | source)
XLA Modules:
  0.0 631.9 jit_solution(2989327285702083715)
XLA Ops:
  8.7 1.5 slice.71
  10.3 3.1 collective-permute-start.1
  13.4 1.5 slice.70
  14.9 3.1 collective-permute-start
  19.1 3.6 collective-permute-done
  22.7 3.4 fusion.35
  26.1 1.7 fusion.6
  27.7 60.7 %all-gather.3.cloned.1.call-done = bf16[384,5120]{0,1:T(8,128)(2,1)} async-done(((bf16[384,320]{0,1:T(8,128)(2,1)}), bf16[384,5120]{0,1:T(8,128)(2,1)}) %all-gather.3.cloned.1.call-update) | async-done | bytes 3932176 | tf_op jit(solution)/shard_map/all_gather | solution.py:80
  88.4 4.6 convolution_convert_fusion.4
  93.0 2.1 multiply_reduce_fusion
  97.3 2.0 fusion.5
  99.3 62.9 %all-gather.5.cloned.1.call-done = bf16[384,5120]{0,1:T(8,128)(2,1)} async-done(((bf16[384,320]{0,1:T(8,128)(2,1)}), bf16[384,5120]{0,1:T(8,128)(2,1)}) %all-gather.5.cloned.1.call-update) | async-done | bytes 3932176 | tf_op jit(solution)/shard_map/all_gather | solution.py:79
  162.2 5.3 fusion.1
  167.6 4.4 copy.70
  172.0 5.3 convolution_convert_fusion
  179.7 5.2 collective-permute-start.3
  187.2 2.5 collective-permute-done.3
  190.8 5.2 fusion.3
  196.0 4.4 copy.74
  200.5 1.6 fusion.4
  202.9 6.6 %collective-permute-start.2 = (bf16[192,256]{0,1:T(8,128)(2,1)}, bf16[192,256]{0,1:T(8,128)(2,1)S(1)}, u32[]{:S(2)}, u32[]{:S(2)}) collective-permute-start(bf16[192,256]{0,1:T(8,128)(2,1)} %bitcast.119), channel_id=1, source_target_pairs={{16,0},{32,16},{48,32},{64,48},{80,64},{96,80},{112,96},{128,112},... | collective-permute-start | bytes 294920 | tf_op jit(solution)/shard_map/ppermute | solution.py:15
  214.2 5.2 fusion.2
  219.3 4.4 copy.72
  224.7 1.5 fusion.40
  226.4 1.5 fusion.41
  228.2 3.4 add_convert_fusion
  231.6 9.4 %reduce-scatter.16.cloned.1.call-done = bf16[320,256]{1,0:T(8,128)(2,1)} async-done(((bf16[5120,256]{1,0:T(8,128)(2,1)}), bf16[320,256]{1,0:T(8,128)(2,1)}) %reduce-scatter.16.cloned.1.call-update) | async-done | bytes 163856
  242.9 86.9 %reduce-scatter.14.cloned.1.call-done = bf16[256,320]{0,1:T(8,128)(2,1)} async-done(((bf16[256,5120]{0,1:T(8,128)(2,1)}), bf16[256,320]{0,1:T(8,128)(2,1)}) %reduce-scatter.14.cloned.1.call-update) | async-done | bytes 163856 | tf_op jit(solution)/shard_map/reduce_scatter | solution.py:134
  329.8 1.7 convert_element_type.113
  331.5 87.0 %reduce-scatter.20.cloned.1.call-done = bf16[320,256]{1,0:T(8,128)(2,1)} async-done(((bf16[5120,256]{1,0:T(8,128)(2,1)}), bf16[320,256]{1,0:T(8,128)(2,1)}) %reduce-scatter.20.cloned.1.call-update) | async-done | bytes 163856
  420.5 86.8 %reduce-scatter.18.cloned.1.call-done = bf16[320,256]{1,0:T(8,128)(2,1)} async-done(((bf16[5120,256]{1,0:T(8,128)(2,1)}), bf16[320,256]{1,0:T(8,128)(2,1)}) %reduce-scatter.18.cloned.1.call-update) | async-done | bytes 163856
  509.1 115.9 %reduce-scatter.12.cloned.1.call-done = bf16[384,320]{0,1:T(8,128)(2,1)} async-done(((bf16[384,5120]{0,1:T(8,128)(2,1)}), bf16[384,320]{0,1:T(8,128)(2,1)}) %reduce-scatter.12.cloned.1.call-update) | async-done | bytes 245776 | tf_op jit(solution)/shard_map/reduce_scatter | solution.py:112
  (65 shorter events, 23.2 us)
Async XLA Ops:
  7.2 216.7 %copy-start = (bf16[5120,256]{1,0:T(8,128)(2,1)S(1)}, bf16[5120,256]{1,0:T(8,128)(2,1)}, u32[]{:S(2)}) copy-start(bf16[5120,256]{1,0:T(8,128)(2,1)} %param.20) | copy-start | bytes 7864324
  7.2 81.2 %all-gather.3.cloned.1.call-start = ((), (), s32[]{:S(2)}) async-start(), calls=%async_computation.5 | async-start | bytes 4177920 | tf_op jit(solution)/shard_map/all_gather | solution.py:80
  7.9 154.3 %all-gather.5.cloned.1.call-start = ((), (), s32[]{:S(2)}) async-start(), calls=%async_computation.7 | async-start | bytes 4177920 | tf_op jit(solution)/shard_map/all_gather | solution.py:79
  8.7 232.3 %reduce-scatter.16.cloned.1.call-start = ((), (), s32[]{:S(2)}) async-start(), calls=%async_computation.9 | async-start | bytes 2785280
  10.3 82.7 %collective-permute-start.1 = (bf16[192,256]{1,0:T(8,128)(2,1)}, bf16[192,256]{1,0:T(8,128)(2,1)}, u32[]{:S(2)}, u32[]{:S(2)}) collective-permute-start(bf16[192,256]{1,0:T(8,128)(2,1)} %slice.71), channel_id=1, source_target_pairs={{0,16},{16,32},{32,48},{48,64},{64,80},{80,96},{96,112},{112,128},... | collective-permute-start | bytes 294920 | tf_op jit(solution)/shard_map/ppermute | solution.py:15
  14.9 7.8 %collective-permute-start = (bf16[192,256]{1,0:T(8,128)(2,1)}, bf16[192,256]{1,0:T(8,128)(2,1)}, u32[]{:S(2)}, u32[]{:S(2)}) collective-permute-start(bf16[192,256]{1,0:T(8,128)(2,1)} %slice.70), channel_id=1, source_target_pairs={{0,16},{16,32},{32,48},{48,64},{64,80},{80,96},{96,112},{112,128},... | collective-permute-start | bytes 294920 | tf_op jit(solution)/shard_map/ppermute | solution.py:15
  88.4 4.6 copy-start.8
  88.4 6.7 %copy-start.4 = (f32[2,384,576]{1,2,0:T(8,128)S(1)}, f32[2,384,576]{1,2,0:T(8,128)}, u32[]{:S(2)}) copy-start(f32[2,384,576]{1,2,0:T(8,128)} %get-tuple-element.45) | copy-start | bytes 5308420
  92.9 3.4 copy-start.7
  95.0 2.2 copy-start.9
  96.4 0.9 copy-start.5
  172.0 157.8 %reduce-scatter.14.cloned.1.call-start = ((), (), s32[]{:S(2)}) async-start(), calls=%async_computation.8 | async-start | bytes 2785280 | tf_op jit(solution)/shard_map/reduce_scatter | solution.py:134
  177.4 241.1 %reduce-scatter.20.cloned.1.call-start = ((), (), s32[]{:S(2)}) async-start(), calls=%async_computation.11 | async-start | bytes 2785280
  178.7 0.8 copy-start.3
  179.7 10.0 %collective-permute-start.3 = (bf16[192,256]{0,1:T(8,128)(2,1)S(1)}, bf16[192,256]{0,1:T(8,128)(2,1)S(1)}, u32[]{:S(2)}, u32[]{:S(2)}) collective-permute-start(bf16[192,256]{0,1:T(8,128)(2,1)S(1)} %bitcast.118), channel_id=1, source_target_pairs={{16,0},{32,16},{48,32},{64,48},{80,64},{96,80},{112,96},{128,112},... | collective-permute-start | bytes 294920 | tf_op jit(solution)/shard_map/ppermute | solution.py:15
  200.5 306.7 %reduce-scatter.18.cloned.1.call-start = ((), (), s32[]{:S(2)}) async-start(), calls=%async_computation.10 | async-start | bytes 2785280
  202.9 10.1 %collective-permute-start.2 = (bf16[192,256]{0,1:T(8,128)(2,1)}, bf16[192,256]{0,1:T(8,128)(2,1)S(1)}, u32[]{:S(2)}, u32[]{:S(2)}) collective-permute-start(bf16[192,256]{0,1:T(8,128)(2,1)} %bitcast.119), channel_id=1, source_target_pairs={{16,0},{32,16},{48,32},{64,48},{80,64},{96,80},{112,96},{128,112},... | collective-permute-start | bytes 294920 | tf_op jit(solution)/shard_map/ppermute | solution.py:15
  223.8 0.9 copy-start.6
  223.8 401.2 %reduce-scatter.12.cloned.1.call-start = ((), (), s32[]{:S(2)}) async-start(), calls=%async_computation.6 | async-start | bytes 4177920 | tf_op jit(solution)/shard_map/reduce_scatter | solution.py:112
  224.7 1.8 copy-start.1
  226.4 1.7 copy-start.2
Sparse Core Ops, SparseCore 0:
  10.7 77.6 all-gather.2
  91.1 71.1 all-gather.4
  172.1 68.8 reduce-scatter.15
  243.3 86.4 reduce-scatter.13
  332.2 86.2 reduce-scatter.19
  420.9 86.2 reduce-scatter.17
  512.2 112.7 reduce-scatter.11
where the time goes:
time: 636 us; the launch traced here: 632 us
  waiting for transfers between devices  517 us (81%)
  matrix products  43.6 us (7%)
  local copies, waits for them, and re-layouts  34.1 us (5%)
  starting transfers between devices  18.3 us (3%)
  between operations  14.4 us (2%)
    unnamed x10, waiting for transfers between devices  185 us
    reduce_scatter x1, waiting for transfers between devices, local(): lax.psum_scatter(partial_sum.astype(jnp.bfloat16), 'tensor', scatter_dime...  116 us
    reduce_scatter x1, waiting for transfers between devices, local(): lax.psum_scatter(part_out.astype(jnp.bfloat16), 'section', scatter_dimens...  86.9 us
    all_gather x1, waiting for transfers between devices, local(): lax.all_gather(layer_input, 'tensor', axis=1, tiled=True)  62.9 us
    all_gather x1, waiting for transfers between devices, local(): lax.all_gather(out_grad, 'tensor', axis=1, tiled=True)  60.7 us
    unnamed x29, local copies, waits for them, and re-layouts  22.1 us
    ppermute x4, starting transfers between devices, from_behind(): return lax.ppermute(x, axis, pairs)  18 us
  transfers between devices with their start and end apart: 11, of which 9 were waited for; matrix products, arithmetic and copies ran while one was open for 11% of the time, Pallas kernels for 0%

commit v1 on v0

v1 whole, which is shorter than its diff:
```python
import math

import jax
import jax.numpy as jnp
from jax import lax
from jax.experimental import pallas as pl
from jax.experimental.pallas import tpu as pltpu
from jax.sharding import PartitionSpec as P

HD = 128
WMAX = 192
ROWS = 384
COLS = 256
SHARD = 320
PAD = 64
KEYS = PAD + WMAX + ROWS
BLOCK = 128
SPAN = 384
SEMS = 160
MESH = pl.DeviceIdType.MESH
BF = jnp.bfloat16
F32 = jnp.float32


def mm(a, b):
    return jnp.dot(a, b, preferred_element_type=F32)


def mm_nt(a, b):
    return lax.dot_general(a, b, (((1,), (1,)), ((), ())), preferred_element_type=F32)


def mm_tn(a, b):
    return lax.dot_general(a, b, (((0,), (0,)), ((), ())), preferred_element_type=F32)


class Wire:
    def __init__(self, send_sem, recv_sem, someone):
        self.send_sem, self.recv_sem, self.someone = send_sem, recv_sem, someone
        self.index = {}
        self.sent = []

    def copy(self, name, src, dst, device):
        i = self.index.setdefault(name, len(self.index))
        assert i < SEMS
        return pltpu.make_async_remote_copy(
            src_ref=src,
            dst_ref=dst,
            send_sem=self.send_sem.at[i],
            recv_sem=self.recv_sem.at[i],
            device_id=device,
            device_id_type=MESH,
        )

    def send(self, name, src, dst, device):
        c = self.copy(name, src, dst, device)
        c.start()
        self.sent.append(c)

    def recv(self, name, dst):
        self.copy(name, dst, dst, self.someone).wait_recv()

    def finish(self):
        for c in self.sent:
            c.wait_send()


def kernel(
    window,
    x_in,
    g_in,
    q_in,
    k_in,
    v_in,
    wq_in,
    wk_in,
    wv_in,
    wo_in,
    ig_out,
    dq_out,
    dk_out,
    dv_out,
    do_out,
    g_all,
    x_all,
    z_rel,
    w_all,
    wo,
    q,
    kcat,
    vcat,
    p_all,
    att,
    hg,
    dq,
    dk,
    dv,
    dk_acc,
    dv_acc,
    halo_out,
    halo_in,
    part,
    rel_l,
    rel_r,
    rec_l,
    rec_r,
    zs,
    zr,
    igp,
    d2r,
    yrel,
    yrec,
    zs_ig,
    zr_ig,
    send_sem,
    recv_sem,
    load_sem,
):
    section = lax.axis_index("section")
    tensor = lax.axis_index("tensor")
    zl, x = section // 4, lax.rem(section, 4)
    zh, y, c = tensor // 8, lax.rem(tensor // 2, 4), lax.rem(tensor, 2)
    zz = zh * 4 + zl
    way = 1 - 2 * c
    xr, xo, xl = lax.rem(x + 1, 4), lax.rem(x + 2, 4), lax.rem(x + 3, 4)
    yr, yo, yl = lax.rem(y + 1, 4), lax.rem(y + 2, 4), lax.rem(y + 3, 4)

    def at(x_=x, y_=y, zz_=zz, c_=c):
        return (lax.rem(zz_, 4) * 4 + x_, (zz_ // 4) * 8 + y_ * 2 + c_)

    def slot(zh_=zh, y_=y, c_=c):
        return zh_ * 8 + y_ * 2 + c_

    def zat(step):
        return at(zz_=lax.rem(zz + step + 8, 8))

    partner = at(c_=1 - c)
    y_right, y_left = at(y_=yr), at(y_=yl)
    x_right, x_left = at(x_=xr), at(x_=xl)
    z_far, z_next = zat(3 * way), zat(way)
    z_low = [(lax.rem(zl + d, 4) * 4 + x, tensor) for d in (1, 2, 3)]
    s_next = (lax.rem(section + 1, 16), tensor)
    s_prev = (lax.rem(section + 15, 16), tensor)

    loads = {}

    def load(name, src, dst):
        cp = pltpu.make_async_copy(src, dst, load_sem.at[len(loads)])
        loads[name] = cp
        cp.start()

    load("q", q_in, q)
    load("k", k_in, kcat.at[pl.ds(PAD + WMAX, ROWS)])
    load("v", v_in, vcat.at[pl.ds(PAD + WMAX, ROWS)])
    load("g", g_in, g_all.at[tensor])
    load("x", x_in, x_all.at[tensor])
    load("wo", wo_in, wo)
    load("wq", wq_in, w_all.at[0])
    load("wk", wk_in, w_all.at[1])
    load("wv", wv_in, w_all.at[2])

    barrier = pltpu.get_barrier_semaphore()
    peers = [partner, y_right, y_left, x_right, x_left, s_next, s_prev]
    peers += z_low + [zat(3), zat(-3), zat(1), zat(-1)]
    for peer in peers:
        pl.semaphore_signal(barrier, inc=1, device_id=peer, device_id_type=MESH)
    pl.semaphore_wait(barrier, len(peers))

    wire = Wire(send_sem, recv_sem, partner)
    send, recv = wire.send, wire.recv

    class Gather:
        def __init__(self, tag, own, buf, rel):
            self.tag, self.own, self.buf, self.rel = tag, own, buf, rel

        def start(self):
            mine = self.buf.at[tensor]
            send(self.tag + "L", self.own, mine, y_right)
            send(self.tag + "R", self.own, mine, y_left)
            send(self.tag + "Q", self.own, self.rel, z_far)
            send(self.tag + "P0", self.own, mine, partner)

        def half(self, s, i):
            return self.buf.at[s, pl.ds(160 * i, 160)]

        def sides(self, z, far, names):
            here = slot(far, yl)
            recv(self.tag + z + "L", self.buf.at[here])
            send(self.tag + z + "OA", self.half(here, 0), self.half(here, 0), y_right)
            send(self.tag + names[0], self.buf.at[here], self.buf.at[here], partner)
            here = slot(far, yr)
            recv(self.tag + z + "R", self.buf.at[here])
            send(self.tag + z + "OB", self.half(here, 1), self.half(here, 1), y_left)
            send(self.tag + names[1], self.buf.at[here], self.buf.at[here], partner)

        def opposite(self, z, far, name):
            here = slot(far, yo)
            recv(self.tag + z + "OA", self.half(here, 0))
            recv(self.tag + z + "OB", self.half(here, 1))
            send(self.tag + name, self.buf.at[here], self.buf.at[here], partner)

        def near_sides(self):
            self.sides("", zh, ("P1", "P2"))

        def near_opposite(self):
            self.opposite("", zh, "P3")

        def relay(self):
            recv(self.tag + "Q", self.rel)
            source = lax.rem(zz - 3 * way + 8, 8)
            here = self.buf.at[slot(source // 4)]
            send(self.tag + "Z", self.rel, here, z_next)

        def across(self):
            here = self.buf.at[slot(1 - zh)]
            recv(self.tag + "Z", here)
            send(self.tag + "ZL", here, here, y_right)
            send(self.tag + "ZR", here, here, y_left)
            send(self.tag + "P4", here, here, partner)

        def far_sides(self):
            self.sides("Z", 1 - zh, ("P5", "P6"))

        def far_opposite(self):
            self.opposite("Z", 1 - zh, "P7")

        def finish(self):
            for i in range(8):
                far = zh if i < 4 else 1 - zh
                where = (y, yl, yr, yo)[i % 4]
                recv(self.tag + "P" + str(i), self.buf.at[slot(far, where, 1 - c)])

    grad = Gather("g", g_in, g_all, z_rel.at[0])
    inp = Gather("x", x_in, x_all, z_rel.at[1])
    halo_rows = pl.ds(ROWS - WMAX, WMAX)
    send("hk", k_in.at[halo_rows], kcat.at[pl.ds(PAD, WMAX)], s_next)
    send("hv", v_in.at[halo_rows], vcat.at[pl.ds(PAD, WMAX)], s_next)
    grad.start()
    inp.start()

    scaling = 1.0 / math.sqrt(HD)
    zero_rows = jnp.zeros((PAD, COLS), BF)
    kcat[pl.ds(0, PAD)] = zero_rows
    vcat[pl.ds(0, PAD)] = zero_rows
    dk_acc[...] = jnp.zeros_like(dk_acc)
    dv_acc[...] = jnp.zeros_like(dv_acc)
    loads["q"].wait()
    loads["k"].wait()
    loads["v"].wait()
    recv("hk", kcat.at[pl.ds(PAD, WMAX)])
    recv("hv", vcat.at[pl.ds(PAD, WMAX)])
    first = section * ROWS

    def forward(b, carry):
        row = pl.multiple_of(b * BLOCK, BLOCK)
        i = lax.broadcasted_iota(jnp.int32, (BLOCK, SPAN), 0)
        j = lax.broadcasted_iota(jnp.int32, (BLOCK, SPAN), 1)
        distance = i + (PAD + WMAX) - j
        key_pos = first - (PAD + WMAX) + row + j
        for h in range(2):
            cols = pl.ds(h * HD, HD)
            keys = kcat[pl.ds(row, SPAN), cols]
            values = vcat[pl.ds(row, SPAN), cols]
            scores = mm_nt(q[pl.ds(row, BLOCK), cols], keys) * scaling
            seen = (distance >= 0) & (distance < window[h]) & (key_pos >= 0)
            scores = jnp.where(seen, scores, -1e30)
            expon = jnp.exp(scores - jnp.max(scores, axis=1, keepdims=True))
            expon = jnp.where(seen, expon, 0.0)
            probs = expon / jnp.sum(expon, axis=1, keepdims=True)
            p_all[h, b] = probs
            att[pl.ds(row, BLOCK), cols] = mm(probs.astype(BF), values).astype(BF)
        return carry

    lax.fori_loop(0, 3, forward, 0)

    grad.near_sides()
    grad.relay()
    inp.near_sides()
    grad.near_opposite()
    grad.across()
    inp.relay()
    inp.near_opposite()
    grad.far_sides()
    grad.far_opposite()
    grad.finish()
    loads["g"].wait()

    def produce(m, a, b):
        def quarter(xq):
            def chunk(j, carry):
                part[m, xq, j] = mm(a[j * 4 + xq], b[...]).astype(BF)
                return carry

            lax.fori_loop(0, 4, chunk, 0)

        tag = "w" + str(m)
        low, high = pl.ds(0, 2), pl.ds(2, 2)
        quarter(xo)
        send(tag + "a", part.at[m, xo, low], rel_l.at[m], x_right)
        send(tag + "b", part.at[m, xo, high], rel_r.at[m], x_left)
        quarter(xr)
        send(tag + "c", part.at[m, xr, high], rec_l.at[m, high], x_right)
        quarter(xl)
        send(tag + "d", part.at[m, xl, low], rec_r.at[m, low], x_left)
        quarter(x)

    def add_relays(m):
        tag = "w" + str(m)
        recv(tag + "a", rel_l.at[m])
        for j in range(2):
            total = part[m, xr, j].astype(F32) + rel_l[m, j].astype(F32)
            part[m, xr, j] = total.astype(BF)
        low, high = pl.ds(0, 2), pl.ds(2, 2)
        send(tag + "e", part.at[m, xr, low], rec_l.at[m, low], x_right)
        recv(tag + "b", rel_r.at[m])
        for j in range(2):
            total = part[m, xl, 2 + j].astype(F32) + rel_r[m, j].astype(F32)
            part[m, xl, 2 + j] = total.astype(BF)
        send(tag + "f", part.at[m, xl, high], rec_r.at[m, high], x_left)

    def sum_x(m):
        tag = "w" + str(m)
        low, high = pl.ds(0, 2), pl.ds(2, 2)
        recv(tag + "c", rec_l.at[m, high])
        recv(tag + "d", rec_r.at[m, low])
        recv(tag + "e", rec_l.at[m, low])
        recv(tag + "f", rec_r.at[m, high])

        def chunk(j, carry):
            total = part[m, x, j].astype(F32) + rec_l[m, j].astype(F32)
            zs[m, j] = (total + rec_r[m, j].astype(F32)).astype(BF)
            return carry

        lax.fori_loop(0, 4, chunk, 0)
        for d in (2, 1, 3):
            send(
                tag + "z" + str(d),
                zs.at[m, lax.rem(zl + d, 4)],
                zr.at[m, d - 1],
                z_low[d - 1],
            )

    def sum_z(m, out):
        for d in (1, 2, 3):
            recv("w" + str(m) + "z" + str(d), zr.at[m, d - 1])
        total = zs[m, zl].astype(F32)
        for d in range(3):
            total = total + zr[m, d].astype(F32)
        out[...] = total

    produce(0, g_all, att)

    loads["wo"].wait()
    head_grad = jnp.zeros((COLS, ROWS), F32)
    for i in range(8):
        head_grad = head_grad + mm(
            wo[:, pl.ds(640 * i, 640)], g_all[pl.ds(2 * i, 2)].reshape(640, ROWS)
        )
    hg[...] = jnp.transpose(head_grad).astype(BF)

    def backward(b, carry):
        row = pl.multiple_of(b * BLOCK, BLOCK)
        for h in range(2):
            cols = pl.ds(h * HD, HD)
            rows, span = pl.ds(row, BLOCK), pl.ds(row, SPAN)
            keys, values = kcat[span, cols], vcat[span, cols]
            grads = hg[rows, cols]
            probs = p_all[h, b]
            prob_grad = mm_nt(grads, values)
            row_term = jnp.sum(
                grads.astype(F32) * att[rows, cols].astype(F32), axis=1, keepdims=True
            )
            score_grad = (probs * (prob_grad - row_term)).astype(BF)
            dq[rows, cols] = (mm(score_grad, keys) * scaling).astype(BF)
            dk_acc[span, cols] += mm_tn(score_grad, q[rows, cols]) * scaling
            dv_acc[span, cols] += mm_tn(probs.astype(BF), grads)
        return carry

    lax.fori_loop(0, 3, backward, 0)
    halo_out[0] = dk_acc[pl.ds(PAD, WMAX)].astype(BF)
    halo_out[1] = dv_acc[pl.ds(PAD, WMAX)].astype(BF)
    send("hg", halo_out, halo_in, s_prev)

    inp.across()
    add_relays(0)
    inp.far_sides()
    inp.far_opposite()
    inp.finish()
    loads["x"].wait()
    produce(1, x_all, dq)

    recv("hg", halo_in)
    for acc, grads, i in ((dk_acc, dk, 0), (dv_acc, dv, 1)):
        own = pl.ds(PAD + WMAX, ROWS - WMAX)
        last = pl.ds(PAD + ROWS, WMAX)
        grads[pl.ds(0, ROWS - WMAX)] = acc[own].astype(BF)
        grads[pl.ds(ROWS - WMAX, WMAX)] = (acc[last] + halo_in[i].astype(F32)).astype(BF)

    sum_x(0)
    add_relays(1)
    produce(2, x_all, dk)

    for name in ("wq", "wk", "wv"):
        loads[name].wait()

    def ig_chunks(core):
        def chunk(j, carry):
            y_, zh_ = j // 2, lax.rem(j, 2)
            s = slot(zh_, y_, core)
            total = mm_nt(w_all[0, s], dq[...])
            total = total + mm_nt(w_all[1, s], dk[...])
            total = total + mm_nt(w_all[2, s], dv[...])
            igp[core, y_, zh_] = total.astype(BF)
            return carry

        lax.fori_loop(0, 8, chunk, 0)

    ig_chunks(1 - c)
    send("id", igp.at[1 - c], d2r, partner)
    ig_chunks(c)

    sum_x(1)
    add_relays(2)
    produce(3, x_all, dv)

    recv("id", d2r)

    def add_core(j, carry):
        y_, zh_ = j // 2, lax.rem(j, 2)
        total = igp[c, y_, zh_].astype(F32) + d2r[y_, zh_].astype(F32)
        igp[c, y_, zh_] = total.astype(BF)
        return carry

    lax.fori_loop(0, 8, add_core, 0)
    send("ia", igp.at[c, yo, 0], yrel.at[0], y_right)
    send("ib", igp.at[c, yo, 1], yrel.at[1], y_left)
    send("ic", igp.at[c, yr, 1], yrec.at[0, 1], y_right)
    send("ie", igp.at[c, yl, 0], yrec.at[1, 0], y_left)

    sum_x(2)
    recv("ia", yrel.at[0])
    igp[c, yr, 0] = (igp[c, yr, 0].astype(F32) + yrel[0].astype(F32)).astype(BF)
    send("if", igp.at[c, yr, 0], yrec.at[0, 0], y_right)
    recv("ib", yrel.at[1])
    igp[c, yl, 1] = (igp[c, yl, 1].astype(F32) + yrel[1].astype(F32)).astype(BF)
    send("ig", igp.at[c, yl, 1], yrec.at[1, 1], y_left)

    add_relays(3)

    recv("ic", yrec.at[0, 1])
    recv("ie", yrec.at[1, 0])
    recv("if", yrec.at[0, 0])
    recv("ig", yrec.at[1, 1])
    for i in range(2):
        total = igp[c, y, i].astype(F32) + yrec[0, i].astype(F32)
        zs_ig[i] = (total + yrec[1, i].astype(F32)).astype(BF)
    send("iq", zs_ig.at[1 - zh], zr_ig.at[0], z_far)

    sum_z(0, do_out)
    recv("iq", zr_ig.at[0])
    send("iz", zr_ig.at[0], zr_ig.at[1], z_next)
    sum_z(1, dq_out)

    sum_x(3)
    recv("iz", zr_ig.at[1])
    ig_out[...] = (zs_ig[zh].astype(F32) + zr_ig[1].astype(F32)).astype(BF)
    sum_z(2, dk_out)
    sum_z(3, dv_out)
    wire.finish()


def local(
    layer_input, query_rows, key_rows, value_rows, out_grad, window, w_query, w_key, w_value, w_out
):
    anywhere = pl.BlockSpec(memory_space=pl.ANY)
    vmem = pl.BlockSpec(memory_space=pltpu.VMEM)
    chunk = (SHARD, COLS)
    outs = pl.pallas_call(
        kernel,
        out_shape=(
            jax.ShapeDtypeStruct((SHARD, ROWS), BF),
            jax.ShapeDtypeStruct(chunk, F32),
            jax.ShapeDtypeStruct(chunk, F32),
            jax.ShapeDtypeStruct(chunk, F32),
            jax.ShapeDtypeStruct(chunk, F32),
        ),
        in_specs=[pl.BlockSpec(memory_space=pltpu.SMEM)] + [anywhere] * 9,
        out_specs=(vmem,) * 5,
        scratch_shapes=[
            pltpu.VMEM((16, SHARD, ROWS), BF),
            pltpu.VMEM((16, SHARD, ROWS), BF),
            pltpu.VMEM((2, SHARD, ROWS), BF),
            pltpu.VMEM((3, 16) + chunk, BF),
            pltpu.VMEM((COLS, 16 * SHARD), BF),
            pltpu.VMEM((ROWS, COLS), BF),
            pltpu.VMEM((KEYS, COLS), BF),
            pltpu.VMEM((KEYS, COLS), BF),
            pltpu.VMEM((2, 3, BLOCK, SPAN), F32),
            pltpu.VMEM((ROWS, COLS), BF),
            pltpu.VMEM((ROWS, COLS), BF),
            pltpu.VMEM((ROWS, COLS), BF),
            pltpu.VMEM((ROWS, COLS), BF),
            pltpu.VMEM((ROWS, COLS), BF),
            pltpu.VMEM((KEYS, COLS), F32),
            pltpu.VMEM((KEYS, COLS), F32),
            pltpu.VMEM((2, WMAX, COLS), BF),
            pltpu.VMEM((2, WMAX, COLS), BF),
            pltpu.VMEM((4, 4, 4) + chunk, BF),
            pltpu.VMEM((4, 2) + chunk, BF),
            pltpu.VMEM((4, 2) + chunk, BF),
            pltpu.VMEM((4, 4) + chunk, BF),
            pltpu.VMEM((4, 4) + chunk, BF),
            pltpu.VMEM((4, 4) + chunk, BF),
            pltpu.VMEM((4, 3) + chunk, BF),
            pltpu.VMEM((2, 4, 2, SHARD, ROWS), BF),
            pltpu.VMEM((4, 2, SHARD, ROWS), BF),
            pltpu.VMEM((2, SHARD, ROWS), BF),
            pltpu.VMEM((2, 2, SHARD, ROWS), BF),
            pltpu.VMEM((2, SHARD, ROWS), BF),
            pltpu.VMEM((2, SHARD, ROWS), BF),
            pltpu.SemaphoreType.DMA((SEMS,)),
            pltpu.SemaphoreType.DMA((SEMS,)),
            pltpu.SemaphoreType.DMA((9,)),
        ],
        compiler_params=pltpu.CompilerParams(
            collective_id=0, has_side_effects=True, vmem_limit_bytes=66_000_000
        ),
        name="layer_backward",
    )(
        window,
        layer_input.T,
        out_grad.T,
        query_rows,
        key_rows,
        value_rows,
        w_query.reshape(16, SHARD, COLS),
        w_key.reshape(16, SHARD, COLS),
        w_value.reshape(16, SHARD, COLS),
        w_out,
    )
    input_grad, query_grad, key_grad, value_grad, out_grad_t = outs
    return (input_grad.T, query_grad, key_grad, value_grad, out_grad_t.T)


def solution(mesh):
    in_specs = (
        P("section", "tensor"),
        P("section", "tensor"),
        P("section", "tensor"),
        P("section", "tensor"),
        P("section", "tensor"),
        P("tensor"),
        P(None, "tensor"),
        P(None, "tensor"),
        P(None, "tensor"),
        P("tensor", None),
    )
    out_specs = (
        P("section", "tensor"),
        P("section", "tensor"),
        P("section", "tensor"),
        P("section", "tensor"),
        P("tensor", "section"),
    )
    return jax.shard_map(local, mesh=mesh, in_specs=in_specs, out_specs=out_specs, check_vma=False)
```

time: 636 us -> 169 us (0.27)
  waiting for transfers between devices: 517 us -> 0 us
  Pallas kernels: 0 us -> 158 us
  matrix products: 43.6 us -> 0 us
  local copies, waits for them, and re-layouts: 34.1 us -> 7.59 us
  starting transfers between devices: 18.3 us -> 0 us
  between operations: 14.4 us -> 0.65 us
    reduce_scatter x2 -> x0, waiting for transfers between devices: 203 us -> none  [the longest x1 116 us: local(): lax.psum_scatter(partial_sum.astype(jnp.bfloat16), 'tensor', scatter_dime...]
    unnamed x10 -> x0, waiting for transfers between devices: 185 us -> none
    pallas_call x0 -> x1, Pallas kernels: none -> 158 us  [local(): pl.pallas_call(kernel, out_shape=(jax.ShapeDtypeStruct((SHARD, ROWS), BF)...]
    all_gather x2 -> x0, waiting for transfers between devices: 124 us -> none  [the longest x1 62.9 us: local(): lax.all_gather(layer_input, 'tensor', axis=1, tiled=True)]
    dot_general x13 -> x0, matrix products: 40.3 us -> none  [the longest x1 5.32 us: local(): lax.dot_general(attended, full_grad, by_rows, preferred_element_type=jnp....]
    ppermute x4 -> x0, starting transfers between devices: 18 us -> none  [from_behind(): return lax.ppermute(x, axis, pairs)]
    unnamed x29 -> x7, local copies, waits for them, and re-layouts: 22.1 us -> 7.59 us
  transfers between devices with their start and end apart: 11 -> 0, of which waited for: 9 -> 0; matrix products, arithmetic and copies ran while one was open for 11% -> 0% of each run, Pallas kernels for 0% -> 0%
where the time goes in v1:
time: 169 us; the launch traced here: 166 us
  Pallas kernels  158 us (93%)
  local copies, waits for them, and re-layouts  7.59 us (4%)
    pallas_call x1, Pallas kernels, local(): pl.pallas_call(kernel, out_shape=(jax.ShapeDtypeStruct((SHARD, ROWS), BF)...  158 us
    unnamed x7, local copies, waits for them, and re-layouts  7.59 us

profile of v1, /device:TPU:33, one launch (start us, length us, event | category | flops | bytes accessed | tf_op | source)
XLA Modules:
  0.0 166.2 jit_solution(16368725122125832697)
XLA Ops:
  0.6 157.9 %layer_backward.1 = (bf16[320,384]{1,0:T(8,128)(2,1)}, f32[320,256]{1,0:T(8,128)}, f32[320,256]{1,0:T(8,128)}, f32[320,256]{1,0:T(8,128)}, f32[320,256]{1,0:T(8,128)}) custom-call(s32[2]{0:T(128)} %window.1, bf16[320,384]{1,0:T(8,128)(2,1)} %bitcast.11, bf16[320,384]{1,0:T(8,128)(2,1)} %bitcast.12, bf16[384,256]{1,0:T(8,128)(2,1)} %q_in.1, ...), custom_call_target="tpu_custom_call" | custom-call | tf_op jit(solution)/shard_map/layer_backward/pallas_call | solution.py:478
  158.6 0.0 copy-start
  158.6 1.7 %copy.20 = bf16[384,320]{0,1:T(8,128)(2,1)} copy(bf16[384,320]{0,1:T(8,128)(2,1)} %bitcast.13) | data formatting | bytes 491520
  160.3 1.7 %copy.21 = f32[320,256]{1,0:T(8,128)} copy(f32[320,256]{1,0:T(8,128)} %get-tuple-element.21) | data formatting | bytes 655360
  162.0 1.7 %copy.22 = f32[320,256]{1,0:T(8,128)} copy(f32[320,256]{1,0:T(8,128)} %get-tuple-element.22) | data formatting | bytes 655360
  163.7 1.7 %copy.23 = f32[320,256]{1,0:T(8,128)} copy(f32[320,256]{1,0:T(8,128)} %get-tuple-element.23) | data formatting | bytes 655360
  165.5 0.0 copy-done
  165.5 0.7 copy.24
Async XLA Ops:
  158.6 6.9 %copy-start = (f32[320,256]{1,0:T(8,128)S(1)}, f32[320,256]{1,0:T(8,128)}, u32[]{:S(2)}) copy-start(f32[320,256]{1,0:T(8,128)} %get-tuple-element.14) | copy-start | bytes 983044

commit v2 on v1

v2 whole, which is shorter than its diff:
```python
import math

import jax
import jax.numpy as jnp
from jax import lax
from jax.experimental import pallas as pl
from jax.experimental.pallas import tpu as pltpu
from jax.sharding import PartitionSpec as P

HD = 128
WMAX = 192
ROWS = 384
COLS = 256
SHARD = 320
PAD = 64
KEYS = PAD + WMAX + ROWS
BLOCK = 128
SPAN = 384
SEMS = 160
MESH = pl.DeviceIdType.MESH
BF = jnp.bfloat16
F32 = jnp.float32


def mm(a, b):
    return jnp.dot(a, b, preferred_element_type=F32)


def mm_nt(a, b):
    return lax.dot_general(a, b, (((1,), (1,)), ((), ())), preferred_element_type=F32)


def mm_tn(a, b):
    return lax.dot_general(a, b, (((0,), (0,)), ((), ())), preferred_element_type=F32)


class Wire:
    def __init__(self, send_sem, recv_sem, someone):
        self.send_sem, self.recv_sem, self.someone = send_sem, recv_sem, someone
        self.index = {}
        self.sent = []
        self.role = None

    def copy(self, name, src, dst, device):
        i = self.index.setdefault(name, len(self.index))
        assert i < SEMS
        return pltpu.make_async_remote_copy(
            src_ref=src,
            dst_ref=dst,
            send_sem=self.send_sem.at[i],
            recv_sem=self.recv_sem.at[i],
            device_id=device,
            device_id_type=MESH,
        )

    def send(self, name, src, dst, device, like=None):
        c = self.copy(name, src, dst, device)
        c.start()
        self.sent.append((self.role, c if like is None else (name, like)))

    def only(self, role, body):
        self.role = role
        pl.when(role)(body)
        self.role = None

    def recv(self, name, dst):
        self.copy(name, dst, dst, self.someone).wait_recv()

    def finish(self):
        for role, c in self.sent:
            if role is None:
                c.wait_send()
            else:

                def body(name=c[0], like=c[1]):
                    self.copy(name, like(), like(), self.someone).wait_send()

                pl.when(role)(body)


def kernel(
    window,
    x_in,
    g_in,
    q_in,
    k_in,
    v_in,
    wq_in,
    wk_in,
    wv_in,
    wo_in,
    ig_out,
    dq_out,
    dk_out,
    dv_out,
    do_out,
    g_all,
    xg,
    z_rel,
    w_all,
    wo,
    q,
    kcat,
    vcat,
    p_all,
    att,
    hg,
    d_all,
    dk_acc,
    dv_acc,
    halo_out,
    halo_in,
    part,
    rel_l,
    rel_r,
    rec_l,
    rec_r,
    pz,
    z1,
    zs,
    z2,
    igp,
    d2r,
    yrel,
    yrec,
    zs_ig,
    zr_ig,
    send_sem,
    recv_sem,
    load_sem,
    home_send,
    home_recv,
):
    section = lax.axis_index("section")
    tensor = lax.axis_index("tensor")
    zl, x = section // 4, lax.rem(section, 4)
    zh, y, c = tensor // 8, lax.rem(tensor // 2, 4), lax.rem(tensor, 2)
    zz = zh * 4 + zl
    way = 1 - 2 * c
    xr, xo, xl = lax.rem(x + 1, 4), lax.rem(x + 2, 4), lax.rem(x + 3, 4)
    yr, yo, yl = lax.rem(y + 1, 4), lax.rem(y + 2, 4), lax.rem(y + 3, 4)

    def at(x_=x, y_=y, zz_=zz, c_=c):
        return (lax.rem(zz_, 4) * 4 + x_, (zz_ // 4) * 8 + y_ * 2 + c_)

    def slot(zh_=zh, y_=y, c_=c):
        return zh_ * 8 + y_ * 2 + c_

    def zat(step, x_=x):
        return at(x_=x_, zz_=lax.rem(zz + step + 8, 8))

    partner = at(c_=1 - c)
    y_right, y_left = at(y_=yr), at(y_=yl)
    x_right, x_left = at(x_=xr), at(x_=xl)
    z_far = zat(3 * way)
    odd = lax.rem(zl, 2)
    z_one = ((zl + 1 - 2 * odd) * 4 + x, tensor)
    z_two = (lax.rem(zl + 2, 4) * 4 + x, tensor)
    s_next = (lax.rem(section + 1, 16), tensor)
    s_prev = (lax.rem(section + 15, 16), tensor)

    home = lax.rem(y, 2) * 2 + c
    to_home = lax.rem(home - x + 4, 4)
    on_core = c == lax.rem(x, 2)
    on_chip = lax.rem(y, 2) == x // 2
    holder = jnp.logical_and(on_core, on_chip)
    middle = jnp.logical_and(on_core, jnp.logical_not(on_chip))
    follower = jnp.logical_not(on_core)
    y_a = jnp.where(on_chip, y, yl)
    y_b = jnp.where(on_chip, yo, yr)

    loads = {}

    def load(name, src, dst):
        cp = pltpu.make_async_copy(src, dst, load_sem.at[len(loads)])
        loads[name] = cp
        cp.start()

    load("q", q_in, q)
    load("k", k_in, kcat.at[pl.ds(PAD + WMAX, ROWS)])
    load("v", v_in, vcat.at[pl.ds(PAD + WMAX, ROWS)])
    load("g", g_in, g_all.at[tensor])
    load("wo", wo_in, wo)
    load("wq", wq_in, w_all.at[0])
    load("wk", wk_in, w_all.at[1])
    load("wv", wv_in, w_all.at[2])
    own_x = pltpu.make_async_copy(x_in, xg.at[zh * 2 + y // 2, x], load_sem.at[len(loads)])
    pl.when(to_home == 0)(own_x.start)

    barrier = pltpu.get_barrier_semaphore()
    peers = [partner, y_right, y_left, x_right, x_left, at(x_=xo), s_next, s_prev]
    peers += [z_one, z_two, zat(3), zat(-3)]
    peers += [zat(step, x_) for step in (1, -1) for x_ in (x, xr, xo, xl)]
    for peer in peers:
        pl.semaphore_signal(barrier, inc=1, device_id=peer, device_id_type=MESH)
    pl.semaphore_wait(barrier, len(peers))

    wire = Wire(send_sem, recv_sem, partner)
    send, recv = wire.send, wire.recv

    class Gather:
        def __init__(self, tag, own, buf, rel):
            self.tag, self.own, self.buf, self.rel = tag, own, buf, rel

        def start(self):
            def own(i):
                return self.own.at[pl.ds(160 * i, 160)]

            for i in range(2):
                send(self.tag + "L" + str(i), own(i), self.half(tensor, i), y_right)
                send(self.tag + "R" + str(i), own(1 - i), self.half(tensor, 1 - i), y_left)
                send(self.tag + "Q" + str(i), own(i), self.rel.at[pl.ds(160 * i, 160)], z_far)
            send(self.tag + "P0", self.own, self.buf.at[tensor], partner)

        def half(self, s, i):
            return self.buf.at[s, pl.ds(160 * i, 160)]

        def sides(self, z, far, names):
            left, right = slot(far, yl), slot(far, yr)
            recv(self.tag + z + "L0", self.half(left, 0))
            send(self.tag + z + "OA", self.half(left, 0), self.half(left, 0), y_right)
            recv(self.tag + z + "R0", self.half(right, 1))
            send(self.tag + z + "OB", self.half(right, 1), self.half(right, 1), y_left)
            recv(self.tag + z + "L1", self.half(left, 1))
            send(self.tag + names[0], self.buf.at[left], self.buf.at[left], partner)
            recv(self.tag + z + "R1", self.half(right, 0))
            send(self.tag + names[1], self.buf.at[right], self.buf.at[right], partner)

        def opposite(self, z, far, name):
            here = slot(far, yo)
            recv(self.tag + z + "OA", self.half(here, 0))
            recv(self.tag + z + "OB", self.half(here, 1))
            send(self.tag + name, self.buf.at[here], self.buf.at[here], partner)

        def near_sides(self):
            self.sides("", zh, ("P1", "P2"))

        def near_opposite(self):
            self.opposite("", zh, "P3")

        def relay(self):
            source = lax.rem(zz - 3 * way + 8, 8)
            here = slot(source // 4)
            for i in range(2):
                piece = self.rel.at[pl.ds(160 * i, 160)]
                recv(self.tag + "Q" + str(i), piece)
                send(self.tag + "Z" + str(i), piece, self.half(here, i), zat(way))

        def across(self):
            here = slot(1 - zh)
            low, high = self.half(here, 0), self.half(here, 1)
            recv(self.tag + "Z0", low)
            send(self.tag + "ZL0", low, low, y_right)
            recv(self.tag + "Z1", high)
            send(self.tag + "ZR0", high, high, y_left)
            send(self.tag + "ZL1", high, high, y_right)
            send(self.tag + "ZR1", low, low, y_left)
            send(self.tag + "P4", self.buf.at[here], self.buf.at[here], partner)

        def far_sides(self):
            self.sides("Z", 1 - zh, ("P5", "P6"))

        def far_opposite(self):
            self.opposite("Z", 1 - zh, "P7")

        def finish(self, first):
            for i in range(first, first + 4):
                far = zh if i < 4 else 1 - zh
                where = (y, yl, yr, yo)[i % 4]
                recv(self.tag + "P" + str(i), self.buf.at[slot(far, where, 1 - c)])

    class Spread:
        def block(self, zh_, y_):
            return zh_ * 2 + y_ // 2

        def two(self):
            return xg.at[0, pl.ds(0, 2)]

        def four(self):
            return xg.at[0]

        def start(self):
            there = (zl * 4 + home, tensor)
            self.own = pltpu.make_async_remote_copy(
                src_ref=x_in,
                dst_ref=xg.at[self.block(zh, y), x],
                send_sem=home_send.at[0],
                recv_sem=home_recv.at[to_home],
                device_id=there,
                device_id_type=MESH,
            )
            pl.when(to_home != 0)(self.own.start)

        def start_far(self):
            send("xQ", x_in, z_rel.at[1], z_far)

        def relay(self):
            recv("xQ", z_rel.at[1])
            source = lax.rem(zz - 3 * way + 8, 8)
            self.far = pltpu.make_async_remote_copy(
                src_ref=z_rel.at[1],
                dst_ref=xg.at[self.block(source // 4, y), x],
                send_sem=home_send.at[1],
                recv_sem=home_recv.at[4 + to_home],
                device_id=zat(way, home),
                device_id_type=MESH,
            )
            self.far.start()

        def arrived(self, block, d, i):
            dst = xg.at[block, lax.rem(x - d + 4, 4)]
            pltpu.make_async_remote_copy(
                src_ref=dst,
                dst_ref=dst,
                send_sem=home_send.at[0],
                recv_sem=home_recv.at[i],
                device_id=partner,
                device_id_type=MESH,
            ).wait_recv()

        def spread(self, near, halves):
            tag = "xn" if near else "xf"
            far = zh if near else 1 - zh
            mine = self.block(far, y)

            def body():
                if 0 in halves:
                    if near:
                        own_x.wait()
                    else:
                        self.arrived(mine, 0, 4)
                    for d in (1, 2, 3):
                        self.arrived(mine, d, d if near else 4 + d)
                for i in halves:
                    half = xg.at[mine, pl.ds(2 * i, 2)]
                    send(tag + "L" + str(i), half, half, y_right, self.two)
                    send(tag + "R" + str(i), half, half, y_left, self.two)
                if 1 in halves:
                    send(tag + "A", xg.at[mine], xg.at[mine], partner, self.four)

            wire.only(holder, body)

        def forward(self, near):
            tag = "xn" if near else "xf"
            far = zh if near else 1 - zh
            left, right = self.block(far, yl), self.block(far, yr)

            def half(block, i):
                return xg.at[block, pl.ds(2 * i, 2)]

            def body():
                recv(tag + "L0", half(left, 0))
                send(tag + "OA", half(left, 0), half(left, 0), y_right, self.two)
                recv(tag + "R0", half(right, 0))
                recv(tag + "L1", half(left, 1))
                recv(tag + "R1", half(right, 1))
                send(tag + "OB", half(right, 1), half(right, 1), y_left, self.two)
                send(tag + "A", xg.at[left], xg.at[left], partner, self.four)
                send(tag + "B", xg.at[right], xg.at[right], partner, self.four)

            wire.only(middle, body)

        def opposite(self, near):
            tag = "xn" if near else "xf"
            far = zh if near else 1 - zh
            here = self.block(far, yo)

            def body():
                recv(tag + "OA", xg.at[here, pl.ds(0, 2)])
                recv(tag + "OB", xg.at[here, pl.ds(2, 2)])
                send(tag + "B", xg.at[here], xg.at[here], partner, self.four)

            wire.only(holder, body)

        def follow(self):
            def body():
                for tag, far in (("xn", zh), ("xf", 1 - zh)):
                    recv(tag + "A", xg.at[self.block(far, y_a)])
                    recv(tag + "B", xg.at[self.block(far, y_b)])

            wire.only(follower, body)

        def finish(self):
            pl.when(to_home != 0)(self.own.wait_send)
            self.far.wait_send()

    grad = Gather("g", g_in, g_all, z_rel.at[0])
    inp = Spread()
    halo_rows = pl.ds(ROWS - WMAX, WMAX)
    grad.start()
    send("hk", k_in.at[halo_rows], kcat.at[pl.ds(PAD, WMAX)], s_next)
    send("hv", v_in.at[halo_rows], vcat.at[pl.ds(PAD, WMAX)], s_next)
    inp.start()
    grad.near_sides()
    grad.relay()
    inp.start_far()
    grad.near_opposite()
    inp.spread(True, (0,))

    scaling = 1.0 / math.sqrt(HD)
    zero_rows = jnp.zeros((PAD, COLS), BF)
    kcat[pl.ds(0, PAD)] = zero_rows
    vcat[pl.ds(0, PAD)] = zero_rows
    dk_acc[...] = jnp.zeros_like(dk_acc)
    dv_acc[...] = jnp.zeros_like(dv_acc)
    loads["q"].wait()
    loads["k"].wait()
    loads["v"].wait()
    recv("hk", kcat.at[pl.ds(PAD, WMAX)])
    recv("hv", vcat.at[pl.ds(PAD, WMAX)])
    first = section * ROWS

    def forward(b, carry):
        row = pl.multiple_of(b * BLOCK, BLOCK)
        i = lax.broadcasted_iota(jnp.int32, (BLOCK, SPAN), 0)
        j = lax.broadcasted_iota(jnp.int32, (BLOCK, SPAN), 1)
        distance = i + (PAD + WMAX) - j
        key_pos = first - (PAD + WMAX) + row + j
        for h in range(2):
            cols = pl.ds(h * HD, HD)
            keys = kcat[pl.ds(row, SPAN), cols]
            values = vcat[pl.ds(row, SPAN), cols]
            scores = mm_nt(q[pl.ds(row, BLOCK), cols], keys) * scaling
            seen = (distance >= 0) & (distance < window[h]) & (key_pos >= 0)
            scores = jnp.where(seen, scores, -1e30)
            expon = jnp.exp(scores - jnp.max(scores, axis=1, keepdims=True))
            expon = jnp.where(seen, expon, 0.0)
            probs = expon / jnp.sum(expon, axis=1, keepdims=True)
            p_all[h, b] = probs
            att[pl.ds(row, BLOCK), cols] = mm(probs.astype(BF), values).astype(BF)
        return carry

    lax.fori_loop(0, 3, forward, 0)

    def out_start(i, tag):
        def quarter(xq):
            def chunk(side, carry):
                part[xq, side, i] = mm(g_all[(i * 2 + side) * 4 + xq], att[...]).astype(BF)
                return carry

            lax.fori_loop(0, 2, chunk, 0)

        quarter(xo)
        send(tag + "a", part.at[xo, 0, i], rel_l.at[i], x_right)
        send(tag + "b", part.at[xo, 1, i], rel_r.at[i], x_left)
        quarter(xr)
        quarter(xl)
        quarter(x)

    def out_rest(i, tag):
        send(tag + "c", part.at[xr, 1, i], rec_l.at[1, i], x_right)
        send(tag + "d", part.at[xl, 0, i], rec_r.at[0, i], x_left)

    def out_relay(i, tag):
        recv(tag + "a", rel_l.at[i])
        total = part[xr, 0, i].astype(F32) + rel_l[i].astype(F32)
        part[xr, 0, i] = total.astype(BF)
        send(tag + "e", part.at[xr, 0, i], rec_l.at[0, i], x_right)
        recv(tag + "b", rel_r.at[i])
        total = part[xl, 1, i].astype(F32) + rel_r[i].astype(F32)
        part[xl, 1, i] = total.astype(BF)
        send(tag + "f", part.at[xl, 1, i], rec_r.at[1, i], x_left)

    def out_sum(i, tag):
        recv(tag + "c", rec_l.at[1, i])
        recv(tag + "d", rec_r.at[0, i])
        recv(tag + "e", rec_l.at[0, i])
        recv(tag + "f", rec_r.at[1, i])

        def chunk(side, carry):
            total = part[x, side, i].astype(F32) + rec_l[side, i].astype(F32)
            pz[0, side, i] = (total + rec_r[side, i].astype(F32)).astype(BF)
            return carry

        lax.fori_loop(0, 2, chunk, 0)
        send("z" + tag, pz.at[0, 1 - odd, i], z1.at[0, i], z_one)

    def share(m):
        mine = d_all.at[m - 1, x]
        send("aL" + str(m), mine, mine, x_right)
        send("aR" + str(m), mine, mine, x_left)

    def share_on(m):
        left, right = d_all.at[m - 1, xl], d_all.at[m - 1, xr]
        recv("aL" + str(m), left)
        half = d_all.at[m - 1, xl, pl.ds(0, 192)]
        send("aA" + str(m), half, half, x_right)
        recv("aR" + str(m), right)
        half = d_all.at[m - 1, xr, pl.ds(192, 192)]
        send("aB" + str(m), half, half, x_left)

    def produce(m):
        recv("aA" + str(m), d_all.at[m - 1, xo, pl.ds(0, 192)])
        recv("aB" + str(m), d_all.at[m - 1, xo, pl.ds(192, 192)])

        def chunks(side):
            def chunk(i, carry):
                total = mm(xg[i * 2 + side, 0], d_all[m - 1, 0])
                for r in range(1, 4):
                    total = total + mm(xg[i * 2 + side, r], d_all[m - 1, r])
                pz[m, side, i] = total.astype(BF)
                return carry

            lax.fori_loop(0, 2, chunk, 0)

        chunks(1 - odd)
        send("z1_" + str(m), pz.at[m, 1 - odd], z1.at[m], z_one)
        chunks(odd)

    def halve(m):
        if m:
            recv("z1_" + str(m), z1.at[m])
        else:
            recv("zn", z1.at[0, zh])
            recv("zf", z1.at[0, 1 - zh])
        other = 1 - zl // 2
        zs[m] = (pz[m, odd, other].astype(F32) + z1[m, other].astype(F32)).astype(BF)
        send("z2_" + str(m), zs.at[m], z2.at[m], z_two)

    def sum_z(m, out):
        recv("z2_" + str(m), z2.at[m])
        total = pz[m, odd, zl // 2].astype(F32) + z1[m, zl // 2].astype(F32)
        out[...] = total + z2[m].astype(F32)

    grad.finish(0)
    loads["g"].wait()
    grad.across()
    out_start(zh, "n")
    out_rest(zh, "n")
    grad.far_sides()
    inp.spread(True, (1,))
    inp.relay()
    out_relay(zh, "n")
    grad.far_opposite()
    grad.finish(4)

    loads["wo"].wait()
    head_grad = jnp.zeros((COLS, ROWS), F32)
    for i in range(8):
        head_grad = head_grad + mm(
            wo[:, pl.ds(640 * i, 640)], g_all[pl.ds(2 * i, 2)].reshape(640, ROWS)
        )
    hg[...] = jnp.transpose(head_grad).astype(BF)

    def backward(b, carry):
        row = pl.multiple_of(b * BLOCK, BLOCK)
        for h in range(2):
            cols = pl.ds(h * HD, HD)
            rows, span = pl.ds(row, BLOCK), pl.ds(row, SPAN)
            keys, values = kcat[span, cols], vcat[span, cols]
            grads = hg[rows, cols]
            probs = p_all[h, b]
            prob_grad = mm_nt(grads, values)
            row_term = jnp.sum(
                grads.astype(F32) * att[rows, cols].astype(F32), axis=1, keepdims=True
            )
            score_grad = (probs * (prob_grad - row_term)).astype(BF)
            d_all[0, x, rows, cols] = (mm(score_grad, keys) * scaling).astype(BF)
            dk_acc[span, cols] += mm_tn(score_grad, q[rows, cols]) * scaling
            dv_acc[span, cols] += mm_tn(probs.astype(BF), grads)
        return carry

    lax.fori_loop(0, 3, backward, 0)
    halo_out[0] = dk_acc[pl.ds(PAD, WMAX)].astype(BF)
    halo_out[1] = dv_acc[pl.ds(PAD, WMAX)].astype(BF)

    share(1)
    send("hg", halo_out, halo_in, s_prev)
    inp.spread(False, (0, 1))
    out_start(1 - zh, "f")
    inp.forward(True)
    out_sum(zh, "n")
    share_on(1)
    inp.opposite(True)
    recv("hg", halo_in)
    for acc, i in ((dk_acc, 0), (dv_acc, 1)):
        own = pl.ds(PAD + WMAX, ROWS - WMAX)
        last = pl.ds(PAD + ROWS, WMAX)
        d_all[1 + i, x, pl.ds(0, ROWS - WMAX)] = acc[own].astype(BF)
        d_all[1 + i, x, pl.ds(ROWS - WMAX, WMAX)] = (acc[last] + halo_in[i].astype(F32)).astype(BF)

    share(2)
    share(3)
    out_rest(1 - zh, "f")

    for name in ("wq", "wk", "wv"):
        loads[name].wait()

    def ig_chunks(core):
        def chunk(j, carry):
            y_, zh_ = j // 2, lax.rem(j, 2)
            s = slot(zh_, y_, core)
            total = mm_nt(w_all[0, s], d_all[0, x])
            total = total + mm_nt(w_all[1, s], d_all[1, x])
            total = total + mm_nt(w_all[2, s], d_all[2, x])
            igp[core, y_, zh_] = total.astype(BF)
            return carry

        lax.fori_loop(0, 8, chunk, 0)

    ig_chunks(1 - c)
    send("id", igp.at[1 - c], d2r, partner)
    inp.forward(False)
    ig_chunks(c)
    inp.opposite(False)
    inp.follow()
    produce(1)
    recv("id", d2r)

    def add_core(j, carry):
        y_, zh_ = j // 2, lax.rem(j, 2)
        total = igp[c, y_, zh_].astype(F32) + d2r[y_, zh_].astype(F32)
        igp[c, y_, zh_] = total.astype(BF)
        return carry

    lax.fori_loop(0, 8, add_core, 0)
    send("ia", igp.at[c, yo, 0], yrel.at[0], y_right)
    send("ib", igp.at[c, yo, 1], yrel.at[1], y_left)
    send("ic", igp.at[c, yr, 1], yrec.at[0, 1], y_right)
    send("ie", igp.at[c, yl, 0], yrec.at[1, 0], y_left)

    share_on(2)
    out_relay(1 - zh, "f")
    produce(2)
    share_on(3)
    recv("ia", yrel.at[0])
    igp[c, yr, 0] = (igp[c, yr, 0].astype(F32) + yrel[0].astype(F32)).astype(BF)
    send("if", igp.at[c, yr, 0], yrec.at[0, 0], y_right)
    recv("ib", yrel.at[1])
    igp[c, yl, 1] = (igp[c, yl, 1].astype(F32) + yrel[1].astype(F32)).astype(BF)
    send("ig", igp.at[c, yl, 1], yrec.at[1, 1], y_left)

    produce(3)
    halve(1)
    out_sum(1 - zh, "f")
    recv("ic", yrec.at[0, 1])
    recv("ie", yrec.at[1, 0])
    recv("if", yrec.at[0, 0])
    recv("ig", yrec.at[1, 1])
    for i in range(2):
        total = igp[c, y, i].astype(F32) + yrec[0, i].astype(F32)
        zs_ig[i] = (total + yrec[1, i].astype(F32)).astype(BF)
    send("iq", zs_ig.at[1 - zh], zr_ig.at[0], z_far)

    halve(2)
    halve(0)
    halve(3)
    sum_z(0, do_out)
    recv("iq", zr_ig.at[0])
    send("iz", zr_ig.at[0], zr_ig.at[1], zat(way))
    sum_z(1, dq_out)
    sum_z(2, dk_out)
    sum_z(3, dv_out)
    recv("iz", zr_ig.at[1])
    ig_out[...] = (zs_ig[zh].astype(F32) + zr_ig[1].astype(F32)).astype(BF)
    inp.finish()
    wire.finish()


def leave(*refs):
    sources, targets, held = refs[:5], refs[5:10], refs[10:15]
    into, out = refs[15:]
    first = [
        pltpu.make_async_copy(s, h, into.at[i]) for i, (s, h) in enumerate(zip(sources, held))
    ]
    second = [
        pltpu.make_async_copy(h, t, out.at[i]) for i, (h, t) in enumerate(zip(held, targets))
    ]
    for cp in first:
        cp.start()
    for a, b in zip(first, second):
        a.wait()
        b.start()
    for cp in second:
        cp.wait()


def local(
    layer_input, query_rows, key_rows, value_rows, out_grad, window, w_query, w_key, w_value, w_out
):
    anywhere = pl.BlockSpec(memory_space=pl.ANY)
    vmem = pl.BlockSpec(memory_space=pltpu.VMEM)
    chunk = (SHARD, COLS)
    outs = pl.pallas_call(
        kernel,
        out_shape=(
            jax.ShapeDtypeStruct((SHARD, ROWS), BF),
            jax.ShapeDtypeStruct(chunk, F32),
            jax.ShapeDtypeStruct(chunk, F32),
            jax.ShapeDtypeStruct(chunk, F32),
            jax.ShapeDtypeStruct(chunk, F32),
        ),
        in_specs=[pl.BlockSpec(memory_space=pltpu.SMEM)] + [anywhere] * 9,
        out_specs=(vmem,) * 5,
        scratch_shapes=[
            pltpu.VMEM((16, SHARD, ROWS), BF),
            pltpu.VMEM((4, 4, SHARD, ROWS), BF),
            pltpu.VMEM((2, SHARD, ROWS), BF),
            pltpu.VMEM((3, 16) + chunk, BF),
            pltpu.VMEM((COLS, 16 * SHARD), BF),
            pltpu.VMEM((ROWS, COLS), BF),
            pltpu.VMEM((KEYS, COLS), BF),
            pltpu.VMEM((KEYS, COLS), BF),
            pltpu.VMEM((2, 3, BLOCK, SPAN), F32),
            pltpu.VMEM((ROWS, COLS), BF),
            pltpu.VMEM((ROWS, COLS), BF),
            pltpu.VMEM((3, 4, ROWS, COLS), BF),
            pltpu.VMEM((KEYS, COLS), F32),
            pltpu.VMEM((KEYS, COLS), F32),
            pltpu.VMEM((2, WMAX, COLS), BF),
            pltpu.VMEM((2, WMAX, COLS), BF),
            pltpu.VMEM((4, 2, 2) + chunk, BF),
            pltpu.VMEM((2,) + chunk, BF),
            pltpu.VMEM((2,) + chunk, BF),
            pltpu.VMEM((2, 2) + chunk, BF),
            pltpu.VMEM((2, 2) + chunk, BF),
            pltpu.VMEM((4, 2, 2) + chunk, BF),
            pltpu.VMEM((4, 2) + chunk, BF),
            pltpu.VMEM((4,) + chunk, BF),
            pltpu.VMEM((4,) + chunk, BF),
            pltpu.VMEM((2, 4, 2, SHARD, ROWS), BF),
            pltpu.VMEM((4, 2, SHARD, ROWS), BF),
            pltpu.VMEM((2, SHARD, ROWS), BF),
            pltpu.VMEM((2, 2, SHARD, ROWS), BF),
            pltpu.VMEM((2, SHARD, ROWS), BF),
            pltpu.VMEM((2, SHARD, ROWS), BF),
            pltpu.SemaphoreType.DMA((SEMS,)),
            pltpu.SemaphoreType.DMA((SEMS,)),
            pltpu.SemaphoreType.DMA((9,)),
            pltpu.SemaphoreType.DMA((2,)),
            pltpu.SemaphoreType.DMA((8,)),
        ],
        compiler_params=pltpu.CompilerParams(
            collective_id=0, has_side_effects=True, vmem_limit_bytes=66_000_000
        ),
        name="layer_backward",
    )(
        window,
        layer_input.T,
        out_grad.T,
        query_rows,
        key_rows,
        value_rows,
        w_query.reshape(16, SHARD, COLS),
        w_key.reshape(16, SHARD, COLS),
        w_value.reshape(16, SHARD, COLS),
        w_out,
    )
    shapes = tuple(jax.ShapeDtypeStruct(o.shape, o.dtype) for o in outs)
    outs = pl.pallas_call(
        leave,
        out_shape=shapes,
        in_specs=[anywhere] * 5,
        out_specs=(anywhere,) * 5,
        scratch_shapes=[pltpu.VMEM(o.shape, o.dtype) for o in outs]
        + [pltpu.SemaphoreType.DMA((5,)), pltpu.SemaphoreType.DMA((5,))],
        name="leave",
    )(*outs)
    input_grad, query_grad, key_grad, value_grad, out_grad_t = outs
    return (input_grad.T, query_grad, key_grad, value_grad, out_grad_t.T)


def solution(mesh):
    in_specs = (
        P("section", "tensor"),
        P("section", "tensor"),
        P("section", "tensor"),
        P("section", "tensor"),
        P("section", "tensor"),
        P("tensor"),
        P(None, "tensor"),
        P(None, "tensor"),
        P(None, "tensor"),
        P("tensor", None),
    )
    out_specs = (
        P("section", "tensor"),
        P("section", "tensor"),
        P("section", "tensor"),
        P("section", "tensor"),
        P("tensor", "section"),
    )
    return jax.shard_map(local, mesh=mesh, in_specs=in_specs, out_specs=out_specs, check_vma=False)
```

time: 169 us -> 131 us (0.78); the launches traced: 166 us -> 130 us
  Pallas kernels: 158 us -> 130 us
  local copies, waits for them, and re-layouts: 7.59 us -> 0 us
    pallas_call x1, Pallas kernels: 158 us -> 127 us  [local(): pl.pallas_call(kernel, out_shape=(jax.ShapeDtypeStruct((SHARD, ROWS), BF)...]
    unnamed x7 -> x0, local copies, waits for them, and re-layouts: 7.59 us -> none
    pallas_call x0 -> x1, Pallas kernels: none -> 2.24 us  [local(): pl.pallas_call(leave, out_shape=shapes, in_specs=[anywhere] * 5, out_spec...]
where the time goes in v2:
time: 131 us; the launch traced here: 130 us
  Pallas kernels  130 us (99%)
    pallas_call x1, Pallas kernels, local(): pl.pallas_call(kernel, out_shape=(jax.ShapeDtypeStruct((SHARD, ROWS), BF)...  127 us

profile of v2, /device:TPU:33, one launch (start us, length us, event | category | flops | bytes accessed | tf_op | source)
XLA Modules:
  0.0 130.3 jit_solution(6239958952409201951)
XLA Ops:
  0.6 127.4 %layer_backward.1 = (bf16[320,384]{1,0:T(8,128)(2,1)}, f32[320,256]{1,0:T(8,128)}, f32[320,256]{1,0:T(8,128)}, f32[320,256]{1,0:T(8,128)}, f32[320,256]{1,0:T(8,128)}) custom-call(s32[2]{0:T(128)} %window.1, bf16[320,384]{1,0:T(8,128)(2,1)} %bitcast.10, bf16[320,384]{1,0:T(8,128)(2,1)} %bitcast.11, bf16[384,256]{1,0:T(8,128)(2,1)} %q_in.1, ...), custom_call_target="tpu_custom_call" | custom-call | tf_op jit(solution)/shard_map/layer_backward/pallas_call | solution.py:684
  128.1 2.2 %leave.1 = (bf16[320,384]{1,0:T(8,128)(2,1)}, f32[320,256]{1,0:T(8,128)}, f32[320,256]{1,0:T(8,128)}, f32[320,256]{1,0:T(8,128)}, f32[320,256]{1,0:T(8,128)}) custom-call(bf16[320,384]{1,0:T(8,128)(2,1)} %get-tuple-element.15.refs_0_, f32[320,256]{1,0:T(8,128)} %get-tuple-element.16.refs_1_, f32[320,256]{1,0:T(8,128)} %get-tuple-element.17.refs_2_, ...), custom_call_target="tpu_custom_call" | custom-call | tf_op jit(solution)/shard_map/leave/pallas_call | solution.py:750

commit v3 on v2

--- a/solution.py
+++ b/solution.py
@@ -105,6 +105,7 @@
     p_all,
     att,
     hg,
+    hg_acc,
     d_all,
     dk_acc,
     dv_acc,
@@ -215,16 +216,18 @@
         def half(self, s, i):
             return self.buf.at[s, pl.ds(160 * i, 160)]
 
-        def sides(self, z, far, names):
+        def sides(self, z, far, names, steps):
             left, right = slot(far, yl), slot(far, yr)
-            recv(self.tag + z + "L0", self.half(left, 0))
-            send(self.tag + z + "OA", self.half(left, 0), self.half(left, 0), y_right)
-            recv(self.tag + z + "R0", self.half(right, 1))
-            send(self.tag + z + "OB", self.half(right, 1), self.half(right, 1), y_left)
-            recv(self.tag + z + "L1", self.half(left, 1))
-            send(self.tag + names[0], self.buf.at[left], self.buf.at[left], partner)
-            recv(self.tag + z + "R1", self.half(right, 0))
-            send(self.tag + names[1], self.buf.at[right], self.buf.at[right], partner)
+            if 0 in steps:
+                recv(self.tag + z + "L0", self.half(left, 0))
+                send(self.tag + z + "OA", self.half(left, 0), self.half(left, 0), y_right)
+                recv(self.tag + z + "R0", self.half(right, 1))
+                send(self.tag + z + "OB", self.half(right, 1), self.half(right, 1), y_left)
+            if 1 in steps:
+                recv(self.tag + z + "L1", self.half(left, 1))
+                send(self.tag + names[0], self.buf.at[left], self.buf.at[left], partner)
+                recv(self.tag + z + "R1", self.half(right, 0))
+                send(self.tag + names[1], self.buf.at[right], self.buf.at[right], partner)
 
         def opposite(self, z, far, name):
             here = slot(far, yo)
@@ -233,7 +236,7 @@
             send(self.tag + name, self.buf.at[here], self.buf.at[here], partner)
 
         def near_sides(self):
-            self.sides("", zh, ("P1", "P2"))
+            self.sides("", zh, ("P1", "P2"), (0, 1))
 
         def near_opposite(self):
             self.opposite("", zh, "P3")
@@ -257,8 +260,8 @@
             send(self.tag + "ZR1", low, low, y_left)
             send(self.tag + "P4", self.buf.at[here], self.buf.at[here], partner)
 
-        def far_sides(self):
-            self.sides("Z", 1 - zh, ("P5", "P6"))
+        def far_sides(self, step):
+            self.sides("Z", 1 - zh, ("P5", "P6"), (step,))
 
         def far_opposite(self):
             self.opposite("Z", 1 - zh, "P7")
@@ -334,13 +337,14 @@
                 for i in halves:
                     half = xg.at[mine, pl.ds(2 * i, 2)]
                     send(tag + "L" + str(i), half, half, y_right, self.two)
+                    half = xg.at[mine, pl.ds(2 - 2 * i, 2)]
                     send(tag + "R" + str(i), half, half, y_left, self.two)
                 if 1 in halves:
                     send(tag + "A", xg.at[mine], xg.at[mine], partner, self.four)
 
             wire.only(holder, body)
 
-        def forward(self, near):
+        def forward(self, near, first):
             tag = "xn" if near else "xf"
             far = zh if near else 1 - zh
             left, right = self.block(far, yl), self.block(far, yr)
@@ -349,14 +353,16 @@
                 return xg.at[block, pl.ds(2 * i, 2)]
 
             def body():
-                recv(tag + "L0", half(left, 0))
-                send(tag + "OA", half(left, 0), half(left, 0), y_right, self.two)
-                recv(tag + "R0", half(right, 0))
-                recv(tag + "L1", half(left, 1))
-                recv(tag + "R1", half(right, 1))
-                send(tag + "OB", half(right, 1), half(right, 1), y_left, self.two)
-                send(tag + "A", xg.at[left], xg.at[left], partner, self.four)
-                send(tag + "B", xg.at[right], xg.at[right], partner, self.four)
+                if first:
+                    recv(tag + "L0", half(left, 0))
+                    send(tag + "OA", half(left, 0), half(left, 0), y_right, self.two)
+                    recv(tag + "R0", half(right, 1))
+                    send(tag + "OB", half(right, 1), half(right, 1), y_left, self.two)
+                else:
+                    recv(tag + "L1", half(left, 1))
+                    send(tag + "A", xg.at[left], xg.at[left], partner, self.four)
+                    recv(tag + "R1", half(right, 0))
+                    send(tag + "B", xg.at[right], xg.at[right], partner, self.four)
 
             wire.only(middle, body)
 
@@ -442,12 +448,12 @@
 
         quarter(xo)
         send(tag + "a", part.at[xo, 0, i], rel_l.at[i], x_right)
-        send(tag + "b", part.at[xo, 1, i], rel_r.at[i], x_left)
         quarter(xr)
         quarter(xl)
         quarter(x)
 
     def out_rest(i, tag):
+        send(tag + "b", part.at[xo, 1, i], rel_r.at[i], x_left)
         send(tag + "c", part.at[xr, 1, i], rec_l.at[1, i], x_right)
         send(tag + "d", part.at[xl, 0, i], rec_r.at[0, i], x_left)
 
@@ -527,20 +533,29 @@
     grad.across()
     out_start(zh, "n")
     out_rest(zh, "n")
-    grad.far_sides()
+
+    loads["wo"].wait()
+
+    def head_grad(z):
+        total = None
+        for i in range(4):
+            cols = pl.ds(pl.multiple_of(z * 2560 + 640 * i, 128), 640)
+            piece = mm(wo[:, cols], g_all[pl.ds(8 * z + 2 * i, 2)].reshape(640, ROWS))
+            total = piece if total is None else total + piece
+        return total
+
+    hg_acc[...] = head_grad(zh)
+    grad.far_sides(0)
+    inp.relay()
+    grad.far_sides(1)
     inp.spread(True, (1,))
-    inp.relay()
     out_relay(zh, "n")
     grad.far_opposite()
+    inp.forward(True, True)
     grad.finish(4)
 
-    loads["wo"].wait()
-    head_grad = jnp.zeros((COLS, ROWS), F32)
-    for i in range(8):
-        head_grad = head_grad + mm(
-            wo[:, pl.ds(640 * i, 640)], g_all[pl.ds(2 * i, 2)].reshape(640, ROWS)
-        )
-    hg[...] = jnp.transpose(head_grad).astype(BF)
+    hg[...] = jnp.transpose(hg_acc[...] + head_grad(1 - zh)).astype(BF)
+    inp.spread(False, (0, 1))
 
     def backward(b, carry):
         row = pl.multiple_of(b * BLOCK, BLOCK)
@@ -564,24 +579,18 @@
     halo_out[0] = dk_acc[pl.ds(PAD, WMAX)].astype(BF)
     halo_out[1] = dv_acc[pl.ds(PAD, WMAX)].astype(BF)
 
+    send("hg", halo_out, halo_in, s_prev)
     share(1)
-    send("hg", halo_out, halo_in, s_prev)
-    inp.spread(False, (0, 1))
     out_start(1 - zh, "f")
-    inp.forward(True)
+    inp.forward(True, False)
+    inp.forward(False, True)
     out_sum(zh, "n")
-    share_on(1)
-    inp.opposite(True)
     recv("hg", halo_in)
     for acc, i in ((dk_acc, 0), (dv_acc, 1)):
         own = pl.ds(PAD + WMAX, ROWS - WMAX)
         last = pl.ds(PAD + ROWS, WMAX)
         d_all[1 + i, x, pl.ds(0, ROWS - WMAX)] = acc[own].astype(BF)
         d_all[1 + i, x, pl.ds(ROWS - WMAX, WMAX)] = (acc[last] + halo_in[i].astype(F32)).astype(BF)
-
-    share(2)
-    share(3)
-    out_rest(1 - zh, "f")
 
     for name in ("wq", "wk", "wv"):
         loads[name].wait()
@@ -598,41 +607,43 @@
 
         lax.fori_loop(0, 8, chunk, 0)
 
-    ig_chunks(1 - c)
-    send("id", igp.at[1 - c], d2r, partner)
-    inp.forward(False)
-    ig_chunks(c)
-    inp.opposite(False)
-    inp.follow()
-    produce(1)
-    recv("id", d2r)
-
     def add_core(j, carry):
         y_, zh_ = j // 2, lax.rem(j, 2)
         total = igp[c, y_, zh_].astype(F32) + d2r[y_, zh_].astype(F32)
         igp[c, y_, zh_] = total.astype(BF)
         return carry
 
+    share(2)
+    inp.opposite(True)
+    ig_chunks(1 - c)
+    send("id", igp.at[1 - c], d2r, partner)
+    share_on(1)
+    share(3)
+    inp.forward(False, False)
+    ig_chunks(c)
+    inp.opposite(False)
+    share_on(2)
+    inp.follow()
+    produce(1)
+    recv("id", d2r)
     lax.fori_loop(0, 8, add_core, 0)
     send("ia", igp.at[c, yo, 0], yrel.at[0], y_right)
     send("ib", igp.at[c, yo, 1], yrel.at[1], y_left)
     send("ic", igp.at[c, yr, 1], yrec.at[0, 1], y_right)
     send("ie", igp.at[c, yl, 0], yrec.at[1, 0], y_left)
-
-    share_on(2)
-    out_relay(1 - zh, "f")
+    share_on(3)
+    out_rest(1 - zh, "f")
     produce(2)
-    share_on(3)
     recv("ia", yrel.at[0])
     igp[c, yr, 0] = (igp[c, yr, 0].astype(F32) + yrel[0].astype(F32)).astype(BF)
     send("if", igp.at[c, yr, 0], yrec.at[0, 0], y_right)
     recv("ib", yrel.at[1])
     igp[c, yl, 1] = (igp[c, yl, 1].astype(F32) + yrel[1].astype(F32)).astype(BF)
     send("ig", igp.at[c, yl, 1], yrec.at[1, 1], y_left)
-
     produce(3)
     halve(1)
-    out_sum(1 - zh, "f")
+    out_relay(1 - zh, "f")
+    halve(2)
     recv("ic", yrec.at[0, 1])
     recv("ie", yrec.at[1, 0])
     recv("if", yrec.at[0, 0])
@@ -641,16 +652,15 @@
         total = igp[c, y, i].astype(F32) + yrec[0, i].astype(F32)
         zs_ig[i] = (total + yrec[1, i].astype(F32)).astype(BF)
     send("iq", zs_ig.at[1 - zh], zr_ig.at[0], z_far)
-
-    halve(2)
+    out_sum(1 - zh, "f")
+    halve(3)
     halve(0)
-    halve(3)
-    sum_z(0, do_out)
     recv("iq", zr_ig.at[0])
     send("iz", zr_ig.at[0], zr_ig.at[1], zat(way))
     sum_z(1, dq_out)
     sum_z(2, dk_out)
     sum_z(3, dv_out)
+    sum_z(0, do_out)
     recv("iz", zr_ig.at[1])
     ig_out[...] = (zs_ig[zh].astype(F32) + zr_ig[1].astype(F32)).astype(BF)
     inp.finish()
@@ -704,6 +714,7 @@
             pltpu.VMEM((2, 3, BLOCK, SPAN), F32),
             pltpu.VMEM((ROWS, COLS), BF),
             pltpu.VMEM((ROWS, COLS), BF),
+            pltpu.VMEM((COLS, ROWS), F32),
             pltpu.VMEM((3, 4, ROWS, COLS), BF),
             pltpu.VMEM((KEYS, COLS), F32),
             pltpu.VMEM((KEYS, COLS), F32),

time: 131 us -> 125 us (0.954)
  Pallas kernels: 130 us -> 122 us
    pallas_call x1, Pallas kernels: 127 us -> 120 us  [local(): pl.pallas_call(kernel, out_shape=(jax.ShapeDtypeStruct((SHARD, ROWS), BF)...]
where the time goes in v3:
time: 125 us; the launch traced here: 123 us
  Pallas kernels  122 us (98%)
    pallas_call x1, Pallas kernels, local(): pl.pallas_call(kernel, out_shape=(jax.ShapeDtypeStruct((SHARD, ROWS), BF)...  120 us

profile of v3, /device:TPU:33, one launch (start us, length us, event | category | flops | bytes accessed | tf_op | source)
XLA Modules:
  0.0 123.1 jit_solution(14032688485612466352)
XLA Ops:
  0.6 120.2 %layer_backward.1 = (bf16[320,384]{1,0:T(8,128)(2,1)}, f32[320,256]{1,0:T(8,128)}, f32[320,256]{1,0:T(8,128)}, f32[320,256]{1,0:T(8,128)}, f32[320,256]{1,0:T(8,128)}) custom-call(s32[2]{0:T(128)} %window.1, bf16[320,384]{1,0:T(8,128)(2,1)} %bitcast.10, bf16[320,384]{1,0:T(8,128)(2,1)} %bitcast.11, bf16[384,256]{1,0:T(8,128)(2,1)} %q_in.1, ...), custom_call_target="tpu_custom_call" | custom-call | tf_op jit(solution)/shard_map/layer_backward/pallas_call | solution.py:694
  120.9 2.2 %leave.1 = (bf16[320,384]{1,0:T(8,128)(2,1)}, f32[320,256]{1,0:T(8,128)}, f32[320,256]{1,0:T(8,128)}, f32[320,256]{1,0:T(8,128)}, f32[320,256]{1,0:T(8,128)}) custom-call(bf16[320,384]{1,0:T(8,128)(2,1)} %get-tuple-element.15.refs_0_, f32[320,256]{1,0:T(8,128)} %get-tuple-element.16.refs_1_, f32[320,256]{1,0:T(8,128)} %get-tuple-element.17.refs_2_, ...), custom_call_target="tpu_custom_call" | custom-call | tf_op jit(solution)/shard_map/leave/pallas_call | solution.py:761

commit v4 on v3

--- a/solution.py
+++ b/solution.py
@@ -620,11 +620,12 @@
     share_on(1)
     share(3)
     inp.forward(False, False)
-    ig_chunks(c)
     inp.opposite(False)
     share_on(2)
+    out_rest(1 - zh, "f")
     inp.follow()
     produce(1)
+    ig_chunks(c)
     recv("id", d2r)
     lax.fori_loop(0, 8, add_core, 0)
     send("ia", igp.at[c, yo, 0], yrel.at[0], y_right)
@@ -632,7 +633,6 @@
     send("ic", igp.at[c, yr, 1], yrec.at[0, 1], y_right)
     send("ie", igp.at[c, yl, 0], yrec.at[1, 0], y_left)
     share_on(3)
-    out_rest(1 - zh, "f")
     produce(2)
     recv("ia", yrel.at[0])
     igp[c, yr, 0] = (igp[c, yr, 0].astype(F32) + yrel[0].astype(F32)).astype(BF)
@@ -640,10 +640,11 @@
     recv("ib", yrel.at[1])
     igp[c, yl, 1] = (igp[c, yl, 1].astype(F32) + yrel[1].astype(F32)).astype(BF)
     send("ig", igp.at[c, yl, 1], yrec.at[1, 1], y_left)
+    out_relay(1 - zh, "f")
+    halve(1)
     produce(3)
-    halve(1)
-    out_relay(1 - zh, "f")
     halve(2)
+    out_sum(1 - zh, "f")
     recv("ic", yrec.at[0, 1])
     recv("ie", yrec.at[1, 0])
     recv("if", yrec.at[0, 0])
@@ -652,7 +653,6 @@
         total = igp[c, y, i].astype(F32) + yrec[0, i].astype(F32)
         zs_ig[i] = (total + yrec[1, i].astype(F32)).astype(BF)
     send("iq", zs_ig.at[1 - zh], zr_ig.at[0], z_far)
-    out_sum(1 - zh, "f")
     halve(3)
     halve(0)
     recv("iq", zr_ig.at[0])

time: 125 us -> 124 us (level); the launches traced: 123 us -> 124 us
  no operation moved by 1% of the time
where the time goes in v4:
time: 124 us
  Pallas kernels  123 us (99%)
    pallas_call x1, Pallas kernels, local(): pl.pallas_call(kernel, out_shape=(jax.ShapeDtypeStruct((SHARD, ROWS), BF)...  121 us

profile of v4, /device:TPU:33, one launch (start us, length us, event | category | flops | bytes accessed | tf_op | source)
XLA Modules:
  0.0 123.6 jit_solution(6066712869309519814)
XLA Ops:
  0.6 120.8 %layer_backward.1 = (bf16[320,384]{1,0:T(8,128)(2,1)}, f32[320,256]{1,0:T(8,128)}, f32[320,256]{1,0:T(8,128)}, f32[320,256]{1,0:T(8,128)}, f32[320,256]{1,0:T(8,128)}) custom-call(s32[2]{0:T(128)} %window.1, bf16[320,384]{1,0:T(8,128)(2,1)} %bitcast.10, bf16[320,384]{1,0:T(8,128)(2,1)} %bitcast.11, bf16[384,256]{1,0:T(8,128)(2,1)} %q_in.1, ...), custom_call_target="tpu_custom_call" | custom-call | tf_op jit(solution)/shard_map/layer_backward/pallas_call | solution.py:694
  121.4 2.2 %leave.1 = (bf16[320,384]{1,0:T(8,128)(2,1)}, f32[320,256]{1,0:T(8,128)}, f32[320,256]{1,0:T(8,128)}, f32[320,256]{1,0:T(8,128)}, f32[320,256]{1,0:T(8,128)}) custom-call(bf16[320,384]{1,0:T(8,128)(2,1)} %get-tuple-element.15.refs_0_, f32[320,256]{1,0:T(8,128)} %get-tuple-element.16.refs_1_, f32[320,256]{1,0:T(8,128)} %get-tuple-element.17.refs_2_, ...), custom_call_target="tpu_custom_call" | custom-call | tf_op jit(solution)/shard_map/leave/pallas_call | solution.py:761

commit v5 on v4

--- a/solution.py
+++ b/solution.py
@@ -634,14 +634,14 @@
     send("ie", igp.at[c, yl, 0], yrec.at[1, 0], y_left)
     share_on(3)
     produce(2)
+    out_relay(1 - zh, "f")
+    halve(1)
     recv("ia", yrel.at[0])
     igp[c, yr, 0] = (igp[c, yr, 0].astype(F32) + yrel[0].astype(F32)).astype(BF)
     send("if", igp.at[c, yr, 0], yrec.at[0, 0], y_right)
     recv("ib", yrel.at[1])
     igp[c, yl, 1] = (igp[c, yl, 1].astype(F32) + yrel[1].astype(F32)).astype(BF)
     send("ig", igp.at[c, yl, 1], yrec.at[1, 1], y_left)
-    out_relay(1 - zh, "f")
-    halve(1)
     produce(3)
     halve(2)
     out_sum(1 - zh, "f")

time: 124 us -> 123 us (level)
  no operation moved by 1% of the time
where the time goes in v5:
time: 123 us
  Pallas kernels  123 us (100%)
    pallas_call x1, Pallas kernels, local(): pl.pallas_call(kernel, out_shape=(jax.ShapeDtypeStruct((SHARD, ROWS), BF)...  120 us

profile of v5, /device:TPU:33, one launch (start us, length us, event | category | flops | bytes accessed | tf_op | source)
XLA Modules:
  0.0 123.3 jit_solution(3706464406506836018)
XLA Ops:
  0.6 120.5 %layer_backward.1 = (bf16[320,384]{1,0:T(8,128)(2,1)}, f32[320,256]{1,0:T(8,128)}, f32[320,256]{1,0:T(8,128)}, f32[320,256]{1,0:T(8,128)}, f32[320,256]{1,0:T(8,128)}) custom-call(s32[2]{0:T(128)} %window.1, bf16[320,384]{1,0:T(8,128)(2,1)} %bitcast.10, bf16[320,384]{1,0:T(8,128)(2,1)} %bitcast.11, bf16[384,256]{1,0:T(8,128)(2,1)} %q_in.1, ...), custom_call_target="tpu_custom_call" | custom-call | tf_op jit(solution)/shard_map/layer_backward/pallas_call | solution.py:694
  121.1 2.2 %leave.1 = (bf16[320,384]{1,0:T(8,128)(2,1)}, f32[320,256]{1,0:T(8,128)}, f32[320,256]{1,0:T(8,128)}, f32[320,256]{1,0:T(8,128)}, f32[320,256]{1,0:T(8,128)}) custom-call(bf16[320,384]{1,0:T(8,128)(2,1)} %get-tuple-element.15.refs_0_, f32[320,256]{1,0:T(8,128)} %get-tuple-element.16.refs_1_, f32[320,256]{1,0:T(8,128)} %get-tuple-element.17.refs_2_, ...), custom_call_target="tpu_custom_call" | custom-call | tf_op jit(solution)/shard_map/leave/pallas_call | solution.py:761
